TPU v7x, 128 devices: a whole 4x4x4 slice. The times are simulated.
128 devices in a mesh: layer: 2 (over core), expert: 16 (over y, x), matrix: 4 (over z).
Axes of the slice: x: 4, y: 4, z: 4, core: 2. Of those that a mesh axis runs over, the one named last changes fastest.
Arguments:
- grads: float32 [32, 1, 2048, 768], P(('layer', 'expert'), None, 'matrix'), parts along dimension 0, may hold values from -6 to 6
- basis_out: float32 [32, 2048, 2048], P('layer', None, ('expert', 'matrix')), parts along dimension 0, may hold values from -0.125 to 0.125
- basis_in: float32 [32, 768, 768], P('layer', ('expert', 'matrix')), parts along dimension 0, may hold values from -0.21875 to 0.21875
- eigvals: float32 [32, 2048, 768], P('layer', ('expert', 'matrix')), parts along dimension 0, may hold values from 0.001 to 1
- counts: int32 [32], P(('layer', 'expert')), parts along dimension 0, may hold values from 0 to 1, as said below
- slot_query: int32 [32, 1], P(('layer', 'expert')), parts along dimension 0, may hold values from 0 to 31
Outputs:
- precond: float32 [32, 1, 2048, 768], P(('layer', 'expert'), None, 'matrix'), parts along dimension 0
- scores: float32 [64], P('layer'), parts along dimension 0
There are 2 independent parts, one for each index of `layer`. A program takes and returns all parts, laid end to end along the dimension named above; each array names one. Nothing has to cross between parts.
Inputs may be any that keep to these rules, and one draw needn't show every extreme that they name: `counts`: some expert has no live slot and some expert has all 1.
All inputs are finite; a program needn't handle non-finite values.
Results may differ from a plain program's by a relative error of at most 0.0003.
Values sent between devices are 32-bit elements; how exact they have to be, the bound alone decides.
A program may use at most 64 MiB of HBM per device.

v0:
```python
import jax
import jax.numpy as jnp
from jax import lax
from jax.sharding import PartitionSpec as P

QUERIES = 32


damping_fixed = 0.05
highest = lax.Precision.HIGHEST


def shards(grads, basis_out, basis_in, eigvals, counts, slot_query):
    capacity = grads.shape[1]
    own_rows = grads.shape[2]
    in_width = grads.shape[3]
    groups = lax.axis_size("matrix")
    columns = lax.all_to_all(basis_out, "expert", split_axis=0, concat_axis=2, tiled=True)[0]
    scales, inner = (
        lax.all_to_all(eigvals, "expert", split_axis=0, concat_axis=1, tiled=True),
        lax.all_to_all(basis_in, "expert", split_axis=0, concat_axis=1, tiled=True),
    )
    inner = lax.all_gather(inner, "matrix", axis=1, tiled=True)[0]
    sources = lax.axis_size("expert")
    inner = inner.reshape(groups, sources, -1, in_width).transpose(1, 0, 2, 3).reshape(-1, in_width)
    divisor = scales[0] + damping_fixed
    live_count = counts[0]
    queries = slot_query[0]
    local_rows = grads[0]
    slot_ids = jnp.arange(capacity, dtype=jnp.int32)
    live = (slot_ids < live_count).astype(jnp.float32)
    rotated = jnp.einsum(
        "ik,if->kf",
        columns,
        lax.all_gather(local_rows[0], "matrix", axis=0, tiled=True),
        precision=highest,
    )
    rotated = jnp.dot(rotated, inner, precision=highest)
    scaled = rotated / divisor
    back = jnp.einsum("kg,hg->kh", scaled, inner, precision=highest)

    def project_one(start, amount, back=back):
        return jnp.dot(columns, back, precision=highest)

    result = lax.psum_scatter(
        project_one(jnp.int32(0), own_rows * lax.axis_size("matrix")),
        "matrix",
        scatter_dimension=0,
        tiled=True,
    )
    results = [result * live[0]]
    precond = jnp.stack(results)
    values = jnp.sum(local_rows * precond, axis=(1, 2)) / (own_rows * groups * in_width)
    targets = jnp.arange(QUERIES, dtype=jnp.int32)
    onehot = (queries[:, None] == targets[None, :]).astype(jnp.float32)
    partial_scores = jnp.sum(values[:, None] * onehot, axis=0)
    scores = lax.psum(partial_scores, ("expert", "matrix"))
    return (precond[None], scores)


def solution(mesh):
    in_specs = (
        P(("layer", "expert"), None, "matrix", None),
        P("layer", None, ("expert", "matrix")),
        P("layer", ("expert", "matrix"), None),
        P("layer", ("expert", "matrix"), None),
        P(("layer", "expert")),
        P(("layer", "expert"), None),
    )
    out_specs = (P(("layer", "expert"), None, "matrix", None), P("layer"))
    return jax.shard_map(shards, mesh=mesh, in_specs=in_specs, out_specs=out_specs, check_vma=False)
```

profile of v0, /device:TPU:0, one launch (start us, length us, event | category | flops | bytes accessed | tf_op | source)
XLA Modules:
  0.0 419.3 jit_solution(11684869709950085901)
XLA Ops:
  7.2 0.0 all-gather.4.cloned.1.call-start
  7.2 1.4 copy.14
  8.6 21.3 %all_to_all.36 = f32[16,12,768]{2,1,0:T(8,128)S(1)} all-to-all(f32[16,12,768]{2,1,0:T(8,128)S(1)} %copy.14), channel_id=1, replica_groups=mesh['layer'=2,'expert'=16,'matrix'=4] {'expert'}, dimensions={0} | all-to-all | bytes 1179648 | tf_op jit(solution)/shard_map/all_to_all | solution.py:21
  29.9 0.9 all_to_all.31
  30.9 0.0 all-gather.4.cloned.1.call-update
  30.9 0.0 all-gather.6.cloned.1.call-start
  30.9 0.7 all-gather.6.cloned.1.call-update
  31.6 0.0 copy-done.2
  31.6 25.2 %all_to_all.37 = f32[16,32,768]{2,1,0:T(8,128)S(1)} all-to-all(f32[16,32,768]{2,1,0:T(8,128)S(1)} %copy-done.2), channel_id=1, replica_groups=mesh['layer'=2,'expert'=16,'matrix'=4] {'expert'}, dimensions={0} | all-to-all | bytes 3145728 | tf_op jit(solution)/shard_map/all_to_all | solution.py:20
  56.8 4.5 %all-to-all-start = ((f32[16,2048,32]{1,2,0:T(8,128)}), f32[16,2048,32]{1,2,0:T(8,128)}, u32[]{:S(2)}, u32[]{:S(2)}) async-start(f32[16,2048,32]{1,2,0:T(8,128)} %param.7), calls=%async_computation | async-start | bytes 8388608 | tf_op jit(solution)/shard_map/all_to_all | solution.py:18
  61.3 0.0 reduce-scatter.2.cloned.1.call-start
  61.4 1.3 broadcast_add_fusion
  62.7 0.0 all-gather.4.cloned.1.call-done
  62.7 2.4 reshape_squeeze.3
  65.1 2.0 copy.15
  67.2 2.6 reshape.33
  69.8 51.2 %all-to-all-done = f32[16,2048,32]{1,2,0:T(8,128)} async-done(((f32[16,2048,32]{1,2,0:T(8,128)}), f32[16,2048,32]{1,2,0:T(8,128)}, u32[]{:S(2)}, u32[]{:S(2)}) %all-to-all-start) | async-done | bytes 4194336 | tf_op jit(solution)/shard_map/all_to_all | solution.py:18
  121.0 9.2 %all-gather.6.cloned.1.call-done = f32[1,1,2048,768]{3,2,1,0:T(8,128)} async-done(((f32[1,1,512,768]{3,2,1,0:T(8,128)}), f32[1,1,2048,768]{3,2,1,0:T(8,128)}) %all-gather.6.cloned.1.call-update) | async-done | bytes 6291472 | tf_op jit(solution)/shard_map/all_gather | solution.py:35
  130.1 0.0 copy-start.1
  130.1 13.4 %fusion = f32[512,768]{1,0:T(8,128)S(1)} fusion(f32[2048,512]{0,1:T(8,128)} %bitcast.2, f32[1,1,2048,768]{3,2,1,0:T(8,128)} %all-gather.6.cloned.1.call-done), kind=kOutput, calls=%fused_computation | convolution fusion | flops 9663676416 | bytes 12058624 | tf_op jit(solution)/shard_map/ik,if->kf/dot_general | solution.py:32
  143.5 0.0 copy-done.1
  143.5 4.1 bitcast_divide_fusion
  147.6 4.0 fusion.3
  151.6 14.2 %convolution_bitcast_fusion = f32[2048,768]{0,1:T(8,128)} fusion(f32[512,768]{1,0:T(8,128)S(1)} %fusion.3, f32[2048,512]{0,1:T(8,128)} %bitcast.2), kind=kOutput, calls=%fused_computation.2 | convolution fusion | flops 9663676416 | bytes 12058624 | tf_op jit(solution)/shard_map/dot_general | solution.py:43
  165.8 0.0 copy-start
  165.8 0.0 reduce-scatter.2.cloned.1.call-update
  165.8 1.4 copy-done
  167.2 0.5 copy.16
  168.9 61.7 %reduce-scatter.2.cloned.1.call-done = f32[512,768]{0,1:T(8,128)} async-done(((f32[2048,768]{0,1:T(8,128)}), f32[512,768]{0,1:T(8,128)}) %reduce-scatter.2.cloned.1.call-update) | async-done | bytes 1572880 | tf_op jit(solution)/shard_map/reduce_scatter | solution.py:45
  230.6 2.5 fusion.2
  233.1 1.6 copy.17
  235.5 177.3 %psum.7 = f32[32]{0:T(128)} all-reduce(f32[32]{0:T(128)S(1)} %compare_select_fusion), channel_id=1, replica_groups=mesh['layer'=2,'expert'=16,'matrix'=4] {'expert','matrix'}, use_global_device_ids=true, to_apply=%region_2.0 | all-reduce | flops 32 | bytes 256 | tf_op jit(solution)/shard_map/psum | solution.py:57
  (2 shorter events, 0.0 us)
Async XLA Ops:
  7.2 55.5 %all-gather.4.cloned.1.call-start = ((), (), s32[]{:S(2)}) async-start(), calls=%async_computation.4 | async-start | bytes 2949120 | tf_op jit(solution)/shard_map/all_gather | solution.py:23
  29.9 1.7 copy-start.2
  30.9 99.2 %all-gather.6.cloned.1.call-start = ((), (), s32[]{:S(2)}) async-start(), calls=%async_computation.6 | async-start | bytes 7864320 | tf_op jit(solution)/shard_map/all_gather | solution.py:35
  56.8 64.2 %all-to-all-start = ((f32[16,2048,32]{1,2,0:T(8,128)}), f32[16,2048,32]{1,2,0:T(8,128)}, u32[]{:S(2)}, u32[]{:S(2)}) async-start(f32[16,2048,32]{1,2,0:T(8,128)} %param.7), calls=%async_computation | async-start | bytes 8388608 | tf_op jit(solution)/shard_map/all_to_all | solution.py:18
  61.3 169.3 %reduce-scatter.2.cloned.1.call-start = ((), (), s32[]{:S(2)}) async-start(), calls=%async_computation.5 | async-start | bytes 7864320 | tf_op jit(solution)/shard_map/reduce_scatter | solution.py:45
  130.1 13.4 %copy-start.1 = (f32[16,32,768]{2,1,0:T(8,128)S(1)}, f32[16,32,768]{2,1,0:T(8,128)}, u32[]{:S(2)}) copy-start(f32[16,32,768]{2,1,0:T(8,128)} %broadcast_add_fusion) | copy-start | bytes 4718596
  165.8 1.4 copy-start
Sparse Core Ops, SparseCore 0:
  31.0 31.6 all-gather.3
  64.3 65.7 all-gather.5
  165.9 64.6 reduce-scatter.1
where the time goes:
time: 420 us; the launch traced here: 419 us
  blocking collectives  224 us (53%)
  waiting for transfers between devices  123 us (29%)
  matrix products  35.6 us (8%)
  between operations  15.8 us (4%)
  local copies, waits for them, and re-layouts  12.9 us (3%)
  starting transfers between devices  4.66 us (1%)
    psum x1, blocking collectives, shards(): scores = lax.psum(partial_scores, ('expert', 'matrix'))  177 us
    reduce_scatter x1, waiting for transfers between devices, shards(): lax.psum_scatter(project_one(jnp.int32(0), own_rows * lax.axis_size('matr...  61.7 us
    all_to_all x1, waiting for transfers between devices, shards(): lax.all_to_all(basis_out, 'expert', split_axis=0, concat_axis=2, tiled=True)  51.2 us
    all_to_all x1, blocking collectives, shards(): lax.all_to_all(eigvals, 'expert', split_axis=0, concat_axis=1, tiled=True)  25.2 us
    all_to_all x1, blocking collectives, shards(): lax.all_to_all(basis_in, 'expert', split_axis=0, concat_axis=1, tiled=True)  21.3 us
    dot_general x1, matrix products, project_one(): return jnp.dot(columns, back, precision=highest)  14.2 us
    dot_general x1, matrix products, shards(): jnp.einsum('ik,if->kf', columns, lax.all_gather(local_rows[0], 'matrix',...  13.4 us
    all_gather x1, waiting for transfers between devices, shards(): lax.all_gather(local_rows[0], 'matrix', axis=0, tiled=True)  9.16 us
  transfers between devices with their start and end apart: 4, of which 3 were waited for; matrix products, arithmetic and copies ran while one was open for 2% of the time, Pallas kernels for 0%

commit v1 on v0

v1 whole, which is shorter than its diff:
```python
import functools

import jax
import jax.numpy as jnp
from jax import lax
from jax.experimental import pallas as pl
from jax.experimental.pallas import tpu as pltpu
from jax.sharding import PartitionSpec as P

MESH = pl.DeviceIdType.MESH
QUERIES = 32
SIDE = 4
PLANES = 4
EXPERTS = 16
DAMPING = 0.05
BF16 = jnp.bfloat16
F32 = jnp.float32

ORDER = [(0, 0)] + sorted(
    [(dy, dx) for dy in range(SIDE) for dx in range(SIDE) if dy or dx],
    key=lambda d: min(d[0], SIDE - d[0]) + min(d[1], SIDE - d[1]),
)
CHUNKS = 4
PER_CHUNK = EXPERTS // CHUNKS


def split(x):
    high = x.astype(BF16)
    return high, (x - high.astype(F32)).astype(BF16)


def dot(a, b):
    return lax.dot_general(a, b, (((1,), (0,)), ((), ())), preferred_element_type=F32)


def dot_t(a, b):
    return lax.dot_general(a, b, (((1,), (1,)), ((), ())), preferred_element_type=F32)


def wait_bytes(ref, sem):
    pltpu.make_async_copy(ref, ref, sem).wait()


def kernel(
    g, bo, bi, lam, counts, query, out, scores,
    g_all, bo_all, bi_all, lam_all, g_hi, g_lo, bo_hi, bo_lo, bi_hi, bi_lo,
    bt_hi, bt_lo, snd, own, rcv, fin, score_acc, scz, scx, scy,
    loc_sem, g_send, g_recv, bi_send, bi_recv, rel_send, rel_recv,
    bo_send, bo_recv, lam_send, lam_recv, out_send, out_recv, fin_sem,
    sc_send, sc_recv,
):
    layer = lax.axis_index("layer")
    e = lax.axis_index("expert")
    m = lax.axis_index("matrix")
    y, x = e // SIDE, lax.rem(e, SIDE)
    active = lax.rem(m + layer, 2) == 0
    rows = g.shape[0]
    piece = bo.shape[1]
    half = piece // 2
    slot_rows = 2 * piece
    chunk_rows = PER_CHUNK * slot_rows
    width = bo.shape[2]
    inner = g.shape[1]
    parts = snd.shape[1]
    tall = snd.shape[2]

    def plane(step):
        return lax.rem(m + step, PLANES)

    def place(d):
        return lax.rem(y + d[0], SIDE) * SIDE + lax.rem(x + d[1], SIDE)

    def remote(src, dst, send, recv, expert, matrix):
        return pltpu.make_async_remote_copy(
            src_ref=src,
            dst_ref=dst,
            send_sem=send,
            recv_sem=recv,
            device_id={"layer": layer, "expert": expert, "matrix": matrix},
            device_id_type=MESH,
        )

    g_steps = {1: 0, 3: 1, 2: 2}

    def send_g(step):
        return remote(g, g_all.at[m], g_send.at[g_steps[step]], g_recv.at[g_steps[step]], e, plane(step))

    bi_own = pltpu.make_async_copy(bi.at[e], bi_all.at[m, e], loc_sem.at[0])
    g_own = pltpu.make_async_copy(g, g_all.at[m], loc_sem.at[1])
    bo_own = pltpu.make_async_copy(bo.at[e], bo_all.at[pl.ds(0, piece)], loc_sem.at[2])
    lam_own = pltpu.make_async_copy(lam.at[e], lam_all.at[pl.ds(0, piece)], loc_sem.at[3])

    bi_own.start()
    for s in range(1, EXPERTS):
        to = place(ORDER[s])
        remote(bi.at[to], bi_all.at[m, e], bi_send, bi_recv, to, m).start()

    def send_slot(s, is_active):
        to = place(ORDER[s])
        chunk = s // PER_CHUNK
        base = s * slot_rows
        if is_active:
            remote(bo.at[to], bo_all.at[pl.ds(base, piece)], bo_send, bo_recv.at[chunk], to, m).start()
            remote(lam.at[to], lam_all.at[pl.ds(base, piece)], lam_send, lam_recv.at[chunk], to, m).start()
        else:
            for which, step in enumerate((1, 3)):
                mine = pl.ds(which * half, half)
                there = pl.ds(base + piece + which * half, half)
                remote(bo.at[to, mine], bo_all.at[there], bo_send, bo_recv.at[chunk], to, plane(step)).start()
                remote(lam.at[to, mine], lam_all.at[there], lam_send, lam_recv.at[chunk], to, plane(step)).start()

    def wait_bi_plane():
        bi_own.wait()
        wait_bytes(bi_all.at[0, pl.ds(0, EXPERTS - 1)], bi_recv)

    def send_relay(step):
        return remote(
            bi_all.at[m], bi_all.at[m], rel_send.at[g_steps[step]], rel_recv.at[g_steps[step]], e, plane(step)
        )

    def score_round(buf, me, index, step):
        copies = []
        for t in range(1, 4):
            if step == "z":
                where = (e, plane(t))
            elif step == "x":
                where = (place((0, t)), m)
            else:
                where = (place((t, 0)), m)
            copies.append(
                remote(buf.at[me], buf.at[me], sc_send.at[3 * index + t - 1], sc_recv.at[3 * index + t - 1], *where)
            )
        return copies

    rounds = [score_round(scz, m, 0, "z"), score_round(scx, x, 1, "x"), score_round(scy, y, 2, "y")]

    def start_all(copies):
        for c in copies:
            c.start()

    def wait_all(copies):
        for c in copies:
            c.wait()

    def total(buf):
        return (buf[0] + buf[1]) + (buf[2] + buf[3])

    def out_copy(step, part, where):
        index = {1: 0, 3: 1, 2: 2}[step]
        return remote(
            snd.at[index, part], rcv.at[where, part], out_send.at[index, part], out_recv.at[where, part], e, plane(step)
        )

    def finish(part, value):
        live = jnp.where(counts[0] > 0, 1.0, 0.0).astype(F32)
        fin[part] = jnp.transpose(value * live)
        pltpu.make_async_copy(fin.at[part], out.at[:, pl.ds(part * tall, tall)], fin_sem.at[part]).start()

    @pl.when(active)
    def _():
        g_own.start()
        bo_own.start()
        lam_own.start()
        send_g(2).start()
        for s in range(1, EXPERTS // 2):
            send_slot(s, True)
        wait_bi_plane()
        send_relay(2).start()
        for s in range(EXPERTS // 2, EXPERTS):
            send_slot(s, True)

        for step in (1, 3, 2):
            send_relay(step).wait_recv()
        lanes = inner // 128
        short = bi.shape[1] // lanes

        def unpack(f, carry):
            for c in range(lanes):
                block = jnp.concatenate(
                    [bi_all[k, f, pl.ds(c * short, short), :] for k in range(PLANES)], axis=0
                )
                high, low = split(block)
                at = pl.ds(pl.multiple_of(f * PLANES * short, PLANES * short), PLANES * short)
                bi_hi[at, pl.ds(c * 128, 128)] = high
                bi_lo[at, pl.ds(c * 128, 128)] = low
            return carry

        lax.fori_loop(0, EXPERTS, unpack, 0)

        g_own.wait()
        for step in (1, 3, 2):
            send_g(step).wait_recv()
        for k in range(PLANES):

            def to_halves(r, carry, k=k):
                at = pl.ds(pl.multiple_of(r * 64, 64), 64)
                high, low = split(g_all[k, at, :])
                into = pl.ds(pl.multiple_of(k * rows + r * 64, 64), 64)
                g_hi[into, :] = high
                g_lo[into, :] = low
                return carry

            lax.fori_loop(0, rows // 64, to_halves, 0)

        score_acc[...] = jnp.zeros_like(score_acc)
        bo_own.wait()
        lam_own.wait()

        def direction(c, carry):
            at = pl.ds(pl.multiple_of(c * chunk_rows, chunk_rows), chunk_rows)

            @pl.when(c == 0)
            def _():
                wait_bytes(bo_all.at[pl.ds(piece, chunk_rows - piece)], bo_recv.at[0])
                wait_bytes(lam_all.at[pl.ds(piece, chunk_rows - piece)], lam_recv.at[0])

            @pl.when(c > 0)
            def _():
                wait_bytes(bo_all.at[pl.ds(0, chunk_rows)], bo_recv.at[c])
                wait_bytes(lam_all.at[pl.ds(0, chunk_rows)], lam_recv.at[c])

            high, low = split(bo_all[at, :])
            bo_hi[at, :] = high
            bo_lo[at, :] = low
            first = dot(high, g_hi[...]) + dot(high, g_lo[...]) + dot(low, g_hi[...])
            high, low = split(first)
            turned = dot(high, bi_hi[...]) + dot(high, bi_lo[...]) + dot(low, bi_hi[...])
            scaled = turned / (lam_all[at, :] + DAMPING)
            score_acc[...] += jnp.sum((turned * scaled).reshape(-1, 8, inner), axis=0)
            high, low = split(scaled)
            back = dot_t(bi_hi[...], high) + dot_t(bi_lo[...], high) + dot_t(bi_hi[...], low)
            high, low = split(back)
            bt_hi[c] = high
            bt_lo[c] = low
            return carry

        lax.fori_loop(0, CHUNKS, direction, 0)

        value = jnp.sum(score_acc[...]) / (rows * PLANES * inner)
        value = jnp.where(counts[0] > 0, value, 0.0)
        lane = lax.broadcasted_iota(jnp.int32, (8, 128), 1)
        scz[m] = jnp.where(lane == query[0], value, 0.0)

        def partial(step, part):
            q = plane(step)
            cols = pl.ds(pl.multiple_of(q * rows, 128), rows)
            acc = jnp.zeros((tall, rows), F32)
            h = pl.ds(part * tall, tall)
            for c in range(CHUNKS):
                ks = pl.ds(c * chunk_rows, chunk_rows)
                ah, al = bt_hi[c, h, :], bt_lo[c, h, :]
                wh, wl = bo_hi[ks, cols], bo_lo[ks, cols]
                acc = acc + (dot(ah, wh) + dot(ah, wl) + dot(al, wh))
            return acc

        pending = []
        for part in range(parts):
            for index, step in enumerate((1, 3, 2)):
                snd[index, part] = partial(step, part)
                for c in pending:
                    c.start()
                pending = [out_copy(step, part, {1: 0, 3: 1, 2: 0}[step])]
            if part == 0:
                start_all(rounds[0])
        own[0] = partial(0, 0)
        for c in pending:
            c.start()
        wait_all(rounds[0])
        scx[x] = total(scz)
        own[1] = partial(0, 1)
        start_all(rounds[1])
        own[2] = partial(0, 2)
        wait_all(rounds[1])
        scy[y] = total(scx)
        for part in range(parts):
            out_copy(2, part, 0).wait_recv()
            finish(part, own[part] + rcv[0, part])
            if part == 0:
                start_all(rounds[2])
        wait_all(rounds[2])
        scores[...] = total(scy)

        wait_bytes(bi_all.at[0, pl.ds(0, EXPERTS - 1)], bi_send)
        send_g(2).wait_send()
        send_relay(2).wait_send()
        wait_bytes(bo_all.at[pl.ds(0, (EXPERTS - 1) * piece)], bo_send)
        wait_bytes(lam_all.at[pl.ds(0, (EXPERTS - 1) * piece)], lam_send)
        for part in range(parts):
            for step in (1, 3, 2):
                out_copy(step, part, 0).wait_send()
        for part in range(parts):
            pltpu.make_async_copy(fin.at[part], out.at[:, pl.ds(part * tall, tall)], fin_sem.at[part]).wait()

    @pl.when(jnp.logical_not(active))
    def _():
        scz[m] = jnp.zeros((8, 128), F32)
        send_g(1).start()
        send_g(3).start()
        for s in range(EXPERTS // 2):
            send_slot(s, False)
        wait_bi_plane()
        send_relay(1).start()
        send_relay(3).start()
        for s in range(EXPERTS // 2, EXPERTS):
            send_slot(s, False)
        start_all(rounds[0])
        wait_all(rounds[0])
        scx[x] = total(scz)
        wait_bytes(bi_all.at[0, pl.ds(0, EXPERTS - 1)], bi_send)
        for step in (1, 3):
            send_g(step).wait_send()
            send_relay(step).wait_send()
        wait_bytes(bo_all.at[pl.ds(0, EXPERTS * piece)], bo_send)
        wait_bytes(lam_all.at[pl.ds(0, EXPERTS * piece)], lam_send)
        start_all(rounds[1])
        wait_all(rounds[1])
        scy[y] = total(scx)
        for part in range(parts):
            out_copy(1, part, 0).wait_recv()
            out_copy(3, part, 1).wait_recv()
            finish(part, rcv[0, part] + rcv[1, part])
            if part == 0:
                start_all(rounds[2])
        wait_all(rounds[2])
        scores[...] = total(scy)
        for part in range(parts):
            pltpu.make_async_copy(fin.at[part], out.at[:, pl.ds(part * tall, tall)], fin_sem.at[part]).wait()


def shards(grads, basis_out, basis_in, eigvals, counts, slot_query):
    rows, inner = grads.shape[2:]
    experts, width, piece = basis_out.shape
    short = basis_in.shape[1]
    lanes = inner // 128
    parts = 3
    tall = inner // parts
    own_k = experts * 2 * piece
    bo = jnp.transpose(basis_out, (0, 2, 1))
    bi = basis_in.reshape(experts, short, lanes, 128).transpose(0, 2, 1, 3).reshape(experts, lanes * short, 128)
    hbm = pl.BlockSpec(memory_space=pl.ANY)
    smem = pl.BlockSpec(memory_space=pltpu.SMEM)
    dma = pltpu.SemaphoreType.DMA
    out, scores = pl.pallas_call(
        kernel,
        out_shape=(
            jax.ShapeDtypeStruct((rows, inner), F32),
            jax.ShapeDtypeStruct((8, 128), F32),
        ),
        in_specs=[hbm, hbm, hbm, hbm, smem, smem],
        out_specs=(hbm, pl.BlockSpec(memory_space=pltpu.VMEM)),
        scratch_shapes=[
            pltpu.VMEM((PLANES, rows, inner), F32),
            pltpu.VMEM((own_k, width), F32),
            pltpu.VMEM((PLANES, experts, lanes * short, 128), F32),
            pltpu.VMEM((own_k, inner), F32),
            pltpu.VMEM((PLANES * rows, inner), BF16),
            pltpu.VMEM((PLANES * rows, inner), BF16),
            pltpu.VMEM((own_k, width), BF16),
            pltpu.VMEM((own_k, width), BF16),
            pltpu.VMEM((inner, inner), BF16),
            pltpu.VMEM((inner, inner), BF16),
            pltpu.VMEM((CHUNKS, inner, own_k // CHUNKS), BF16),
            pltpu.VMEM((CHUNKS, inner, own_k // CHUNKS), BF16),
            pltpu.VMEM((3, parts, tall, rows), F32),
            pltpu.VMEM((parts, tall, rows), F32),
            pltpu.VMEM((2, parts, tall, rows), F32),
            pltpu.VMEM((parts, rows, tall), F32),
            pltpu.VMEM((8, inner), F32),
            pltpu.VMEM((4, 8, 128), F32),
            pltpu.VMEM((4, 8, 128), F32),
            pltpu.VMEM((4, 8, 128), F32),
            dma((4,)),
            dma((3,)),
            dma((3,)),
            dma(()),
            dma(()),
            dma((3,)),
            dma((3,)),
            dma(()),
            dma((CHUNKS,)),
            dma(()),
            dma((CHUNKS,)),
            dma((3, parts)),
            dma((2, parts)),
            dma((parts,)),
            dma((9,)),
            dma((9,)),
        ],
        compiler_params=pltpu.CompilerParams(has_side_effects=True, vmem_limit_bytes=66_000_000),
        name="precondition",
    )(grads[0, 0], bo, bi, eigvals, counts, slot_query[0])
    return out[None, None], scores[0, :QUERIES]


def solution(mesh):
    in_specs = (
        P(("layer", "expert"), None, "matrix", None),
        P("layer", None, ("expert", "matrix")),
        P("layer", ("expert", "matrix"), None),
        P("layer", ("expert", "matrix"), None),
        P(("layer", "expert")),
        P(("layer", "expert"), None),
    )
    out_specs = (P(("layer", "expert"), None, "matrix", None), P("layer"))
    return jax.shard_map(shards, mesh=mesh, in_specs=in_specs, out_specs=out_specs, check_vma=False)
```

time: 420 us -> 164 us (0.39)
  blocking collectives: 224 us -> 0 us
  Pallas kernels: 0 us -> 156 us
  waiting for transfers between devices: 123 us -> 0 us
  matrix products: 35.6 us -> 0 us
  between operations: 15.8 us -> 1.94 us
  local copies, waits for them, and re-layouts: 12.9 us -> 6.11 us
  starting transfers between devices: 4.66 us -> 0 us
    psum x1 -> x0, blocking collectives: 177 us -> none  [shards(): scores = lax.psum(partial_scores, ('expert', 'matrix'))]
    pallas_call x0 -> x1, Pallas kernels: none -> 156 us  [shards(): pl.pallas_call(kernel, out_shape=(jax.ShapeDtypeStruct((rows, inner), F32...]
    reduce_scatter x1 -> x0, waiting for transfers between devices: 61.7 us -> none  [shards(): lax.psum_scatter(project_one(jnp.int32(0), own_rows * lax.axis_size('matr...]
    all_to_all x1 -> x0, waiting for transfers between devices: 51.2 us -> none  [shards(): lax.all_to_all(basis_out, 'expert', split_axis=0, concat_axis=2, tiled=True)]
    all_to_all x2 -> x0, blocking collectives: 46.4 us -> none  [the longest x1 25.2 us: shards(): lax.all_to_all(eigvals, 'expert', split_axis=0, concat_axis=1, tiled=True)]
    dot_general x4 -> x0, matrix products: 35.6 us -> none  [the longest x1 14.2 us: project_one(): return jnp.dot(columns, back, precision=highest)]
    all_gather x2 -> x0, waiting for transfers between devices: 9.16 us -> none  [the longest x1 9.16 us: shards(): lax.all_gather(local_rows[0], 'matrix', axis=0, tiled=True)]
    all_to_all x1 -> x0, starting transfers between devices: 4.54 us -> none  [shards(): lax.all_to_all(basis_out, 'expert', split_axis=0, concat_axis=2, tiled=True)]
  transfers between devices with their start and end apart: 4 -> 0, of which waited for: 3 -> 0; matrix products, arithmetic and copies ran while one was open for 2% -> 0% of each run, Pallas kernels for 0% -> 0%
where the time goes in v1:
time: 164 us
  Pallas kernels  156 us (95%)
  local copies, waits for them, and re-layouts  6.11 us (4%)
  between operations  1.94 us (1%)
    pallas_call x1, Pallas kernels, shards(): pl.pallas_call(kernel, out_shape=(jax.ShapeDtypeStruct((rows, inner), F32...  156 us

profile of v1, /device:TPU:0, one launch (start us, length us, event | category | flops | bytes accessed | tf_op | source)
XLA Modules:
  0.0 163.6 jit_solution(1970784101025906460)
XLA Ops:
  1.9 1.2 reshape.10
  3.1 0.1 copy.9
  3.2 1.0 copy.10.bi
  4.2 155.6 %precondition.1 = (f32[512,768]{1,0:T(8,128)}, f32[8,128]{1,0:T(8,128)}) custom-call(f32[512,768]{1,0:T(8,128)} %bitcast.15, f32[16,32,2048]{2,1,0:T(8,128)} %bitcast.11, f32[16,72,128]{2,1,0:T(8,128)} %copy.10.bi, f32[16,32,768]{2,1,0:T(8,128)} %lam.1, s32[1]{0:T(128)S(6)} %copy.12.counts, s32[1]{0:T(128)} %bitcast.10.query), custom_call_target="tpu_custom_call" | custom-call | tf_op jit(solution)/shard_map/precondition/pallas_call | solution.py:343
  159.8 1.2 slice_bitcast_fusion
  161.0 2.7 %copy.14 = f32[1,1,512,768]{3,2,1,0:T(8,128)} copy(f32[1,1,512,768]{3,2,1,0:T(8,128)} %bitcast.14) | data formatting | bytes 3145728

commit v2 on v1

v2 whole, which is shorter than its diff:
```python
import functools

import jax
import jax.numpy as jnp
from jax import lax
from jax.experimental import pallas as pl
from jax.experimental.pallas import tpu as pltpu
from jax.sharding import PartitionSpec as P

MESH = pl.DeviceIdType.MESH
QUERIES = 32
SIDE = 4
PLANES = 4
EXPERTS = 16
DAMPING = 0.05
BF16 = jnp.bfloat16
F32 = jnp.float32

ORDER = [
    (0, 0), (3, 1), (1, 0), (0, 2), (2, 3), (1, 1), (0, 1), (2, 0),
    (0, 3), (3, 0), (1, 2), (3, 3), (1, 3), (2, 1), (3, 2), (2, 2),
]
OWN_CHUNKS = 2
SIDE_CHUNKS = 4
CHUNKS = OWN_CHUNKS + SIDE_CHUNKS


def split(x):
    high = x.astype(BF16)
    return high, (x - high.astype(F32)).astype(BF16)


def dot(a, b):
    return lax.dot_general(a, b, (((1,), (0,)), ((), ())), preferred_element_type=F32)


def dot_t(a, b):
    return lax.dot_general(a, b, (((1,), (1,)), ((), ())), preferred_element_type=F32)


def wait_bytes(ref, sem):
    pltpu.make_async_copy(ref, ref, sem).wait()


def three_pass(product, high, low, other_high, other_low):
    n = high.shape[0]
    both = product(jnp.concatenate([high, low], axis=0), other_high)
    return both[:n] + both[n:] + product(high, other_low)


def kernel(
    g, bo, bi, lam, counts, query, out, scores,
    g_all, bo_all, bi_raw, bi_stage, bi_all, lam_all, g_hi, g_lo, bo_hi, bo_lo, bi_hi, bi_lo,
    back_hi, back_lo, snd, score_acc, scz, scx, scy,
    loc_sem, g_send, g_recv, bi_send, bi_recv, rel_send, rel_recv,
    bo_send, bo_recv, lam_send, lam_recv, hop_send, hop_recv, out_send, out_recv, own_sem,
    sc_send, sc_recv,
):
    layer = lax.axis_index("layer")
    e = lax.axis_index("expert")
    m = lax.axis_index("matrix")
    y, x = e // SIDE, lax.rem(e, SIDE)
    active = lax.rem(m + layer, 2) == 0
    rows = g.shape[0]
    piece = bo.shape[1]
    half = piece // 2
    own_rows = EXPERTS * piece // OWN_CHUNKS
    side_rows = EXPERTS * piece // SIDE_CHUNKS
    inner = g.shape[1]
    parts = snd.shape[1]
    tall = snd.shape[2]
    lanes = inner // 128
    short = bi.shape[0]

    def plane(step):
        return lax.rem(m + step, PLANES)

    def place(d):
        return lax.rem(y + d[0], SIDE) * SIDE + lax.rem(x + d[1], SIDE)

    def remote(src, dst, send, recv, expert, matrix):
        return pltpu.make_async_remote_copy(
            src_ref=src,
            dst_ref=dst,
            send_sem=send,
            recv_sem=recv,
            device_id={"layer": layer, "expert": expert, "matrix": matrix},
            device_id_type=MESH,
        )

    bi_in = pltpu.make_async_copy(bi, bi_raw, loc_sem.at[0])
    bi_in.start()

    barrier = pltpu.get_barrier_semaphore()
    partners = [(e, plane(t)) for t in (1, 3, 2)]
    partners += [(lax.rem(e + s, EXPERTS), m) for s in range(1, EXPERTS)]
    for expert, matrix in partners:
        pl.semaphore_signal(
            barrier,
            inc=1,
            device_id={"layer": layer, "expert": expert, "matrix": matrix},
            device_id_type=MESH,
        )

    bi_in.wait()
    for to in range(EXPERTS):
        for c in range(lanes):
            bi_stage[to, pl.ds(c * short, short), :] = bi_raw[:, to, pl.ds(c * 128, 128)]

    pl.semaphore_wait(barrier, len(partners))

    steps = {1: 0, 3: 1, 2: 2}

    def send_g(step):
        return remote(g, g_all.at[m], g_send.at[steps[step]], g_recv.at[steps[step]], e, plane(step))

    g_own = pltpu.make_async_copy(g, g_all.at[m], loc_sem.at[1])
    bo_own = pltpu.make_async_copy(bo.at[e], bo_all.at[pl.ds(0, piece)], loc_sem.at[2])
    lam_own = pltpu.make_async_copy(lam.at[e], lam_all.at[pl.ds(0, piece)], loc_sem.at[3])

    def send_bi():
        for s in range(1, EXPERTS):
            to = place(ORDER[s])
            remote(bi_stage.at[to], bi_all.at[m, e], bi_send, bi_recv, to, m).start()

    def send_slot(s, is_active):
        to = place(ORDER[s])
        if is_active:
            chunk = s * OWN_CHUNKS // EXPERTS
            there = pl.ds(s * piece, piece)
            remote(bo.at[to], bo_all.at[there], bo_send, bo_recv.at[chunk], to, m).start()
            remote(lam.at[to], lam_all.at[there], lam_send, lam_recv.at[chunk], to, m).start()
        else:
            chunk = s * SIDE_CHUNKS // EXPERTS
            for which in range(2):
                mine = pl.ds(which * half, half)
                there = pl.ds((which * EXPERTS + s) * half, half)
                if s:
                    remote(bo.at[to, mine], bo_all.at[there], bo_send, hop_recv.at[0, chunk], to, m).start()
                    remote(lam.at[to, mine], lam_all.at[there], lam_send, hop_recv.at[1, chunk], to, m).start()
                else:
                    pltpu.make_async_copy(bo.at[e, mine], bo_all.at[there], loc_sem.at[which]).start()
                    pltpu.make_async_copy(lam.at[e, mine], lam_all.at[there], loc_sem.at[2 + which]).start()

    def wait_slots(chunk):
        ready = side_rows
        if chunk == 0:
            ready -= piece
            for which in range(2):
                wait_bytes(bo_all.at[pl.ds(0, half)], loc_sem.at[which])
                wait_bytes(lam_all.at[pl.ds(0, half)], loc_sem.at[2 + which])
        wait_bytes(bo_all.at[pl.ds(0, ready)], hop_recv.at[0, chunk])
        wait_bytes(lam_all.at[pl.ds(0, ready)], hop_recv.at[1, chunk])

    def hand_on(chunk):
        count = side_rows // 2
        for which, step in enumerate((1, 3)):
            here = pl.ds(which * EXPERTS * half + chunk * count, count)
            there = pl.ds(EXPERTS * piece + chunk * side_rows + which * count, count)
            at = OWN_CHUNKS + chunk
            remote(bo_all.at[here], bo_all.at[there], hop_send.at[0, which], bo_recv.at[at], e, plane(step)).start()
            remote(lam_all.at[here], lam_all.at[there], hop_send.at[1, which], lam_recv.at[at], e, plane(step)).start()

    def wait_bi_plane():
        for c in range(lanes):
            bi_all[m, e, pl.ds(c * short, short), :] = bi_stage[e, pl.ds(c * short, short), :]
        wait_bytes(bi_stage.at[pl.ds(0, EXPERTS - 1)], bi_recv)

    def send_relay(step):
        return remote(
            bi_all.at[m], bi_all.at[m], rel_send.at[steps[step]], rel_recv.at[steps[step]], e, plane(step)
        )

    def score_round(buf, me, index, step):
        copies = []
        for t in range(1, 4):
            if step == "z":
                where = (e, plane(t))
            elif step == "x":
                where = (place((0, t)), m)
            else:
                where = (place((t, 0)), m)
            at = 3 * index + t - 1
            copies.append(remote(buf.at[me], buf.at[me], sc_send.at[at], sc_recv.at[at], *where))
        return copies

    rounds = [score_round(scz, m, 0, "z"), score_round(scx, x, 1, "x"), score_round(scy, y, 2, "y")]

    def start_all(copies):
        for c in copies:
            c.start()

    def wait_all(copies):
        for c in copies:
            c.wait()

    def total(buf):
        return (buf[0] + buf[1]) + (buf[2] + buf[3])

    halves = {1: 0, 3: 1, 2: 0}

    def out_copy(step, part):
        index, to = steps[step], halves[step]
        there = out.at[to, pl.ds(part * tall, tall)]
        return remote(
            snd.at[index, part], there, out_send.at[index, part], out_recv.at[to, part], e, plane(step)
        )

    def own_copy(part):
        return pltpu.make_async_copy(snd.at[3, part], out.at[1, pl.ds(part * tall, tall)], own_sem.at[part])

    @pl.when(active)
    def _():
        g_own.start()
        bo_own.start()
        lam_own.start()
        send_g(2).start()
        send_bi()
        for s in range(1, EXPERTS):
            send_slot(s, True)
        wait_bi_plane()
        send_relay(2).start()

        g_own.wait()
        for step in (1, 3, 2):
            send_g(step).wait_recv()
        for k in range(PLANES):

            def to_halves(r, carry, k=k):
                at = pl.ds(pl.multiple_of(r * 64, 64), 64)
                high, low = split(g_all[k, at, :])
                into = pl.ds(pl.multiple_of(k * rows + r * 64, 64), 64)
                g_hi[into, :] = high
                g_lo[into, :] = low
                return carry

            lax.fori_loop(0, rows // 64, to_halves, 0)

        for step in (1, 3, 2):
            send_relay(step).wait_recv()

        def unpack(f, carry):
            for c in range(lanes):
                block = jnp.concatenate(
                    [bi_all[k, f, pl.ds(c * short, short), :] for k in range(PLANES)], axis=0
                )
                high, low = split(block)
                at = pl.ds(pl.multiple_of(f * PLANES * short, PLANES * short), PLANES * short)
                bi_hi[at, pl.ds(c * 128, 128)] = high
                bi_lo[at, pl.ds(c * 128, 128)] = low
            return carry

        lax.fori_loop(0, EXPERTS, unpack, 0)

        score_acc[...] = jnp.zeros_like(score_acc)
        bo_own.wait()
        lam_own.wait()

        def direction(start, size):
            at = pl.ds(start, size)
            columns = bo_all[at, :]
            high, low = split(columns)
            first = three_pass(dot, high, low, g_hi[...], g_lo[...])
            high, low = split(first)
            turned = three_pass(dot, high, low, bi_hi[...], bi_lo[...])
            scaled = turned / (lam_all[at, :] + DAMPING)
            score_acc[...] += jnp.sum((turned * scaled).reshape(-1, 8, inner), axis=0)
            high, low = split(scaled)
            high, low = split(three_pass(dot_t, high, low, bi_hi[...], bi_lo[...]))
            back_hi[at, :] = high
            back_lo[at, :] = low
            high, low = split(jnp.transpose(columns))
            bo_hi[:, at] = high
            bo_lo[:, at] = low

        def own_chunk(c, carry):
            @pl.when(c == 0)
            def _():
                wait_bytes(bo_all.at[pl.ds(piece, own_rows - piece)], bo_recv.at[0])
                wait_bytes(lam_all.at[pl.ds(piece, own_rows - piece)], lam_recv.at[0])

            @pl.when(c > 0)
            def _():
                wait_bytes(bo_all.at[pl.ds(0, own_rows)], bo_recv.at[c])
                wait_bytes(lam_all.at[pl.ds(0, own_rows)], lam_recv.at[c])

            direction(pl.multiple_of(c * own_rows, own_rows), own_rows)
            return carry

        def side_chunk(c, carry):
            wait_bytes(bo_all.at[pl.ds(0, side_rows)], bo_recv.at[OWN_CHUNKS + c])
            wait_bytes(lam_all.at[pl.ds(0, side_rows)], lam_recv.at[OWN_CHUNKS + c])
            direction(pl.multiple_of(EXPERTS * piece + c * side_rows, side_rows), side_rows)
            return carry

        lax.fori_loop(0, OWN_CHUNKS, own_chunk, 0)
        lax.fori_loop(0, SIDE_CHUNKS, side_chunk, 0)

        value = jnp.sum(score_acc[...]) / (rows * PLANES * inner)
        value = jnp.where(counts[0] > 0, value, 0.0)
        lane = lax.broadcasted_iota(jnp.int32, (8, 128), 1)
        scz[m] = jnp.where(lane == query[0], value, 0.0)

        def partial(step, part):
            at = pl.ds(pl.multiple_of(plane(step) * rows + part * tall, tall), tall)
            return three_pass(dot, bo_hi[at, :], bo_lo[at, :], back_hi[...], back_lo[...])

        pending = rounds[0]
        for part in range(parts):
            for index, step in enumerate((1, 3, 2)):
                snd[index, part] = partial(step, part)
                start_all(pending)
                pending = [out_copy(step, part)]
        snd[3, 0] = partial(0, 0)
        start_all(pending)
        wait_all(rounds[0])
        scx[x] = total(scz)
        snd[3, 1] = partial(0, 1)
        start_all(rounds[1])
        own_copy(0).start()
        wait_all(rounds[1])
        scy[y] = total(scx)
        for part in range(2, parts):
            snd[3, part] = partial(0, part)
            own_copy(part - 1).start()
        start_all(rounds[2])
        wait_all(rounds[2])
        scores[...] = total(scy)
        own_copy(parts - 1).start()

        wait_bytes(bi_stage.at[pl.ds(0, EXPERTS - 1)], bi_send)
        send_g(2).wait_send()
        send_relay(2).wait_send()
        wait_bytes(bo_all.at[pl.ds(0, (EXPERTS - 1) * piece)], bo_send)
        wait_bytes(lam_all.at[pl.ds(0, (EXPERTS - 1) * piece)], lam_send)
        for part in range(parts):
            for step in (1, 3, 2):
                out_copy(step, part).wait_send()
            own_copy(part).wait()
            out_copy(2, part).wait_recv()

    @pl.when(jnp.logical_not(active))
    def _():
        scz[m] = jnp.zeros((8, 128), F32)
        send_g(1).start()
        send_g(3).start()
        send_bi()
        for s in range(EXPERTS):
            send_slot(s, False)
        wait_bi_plane()
        send_relay(1).start()
        send_relay(3).start()
        for chunk in range(SIDE_CHUNKS):
            wait_slots(chunk)
            hand_on(chunk)
        start_all(rounds[0])
        wait_all(rounds[0])
        scx[x] = total(scz)
        wait_bytes(bi_stage.at[pl.ds(0, EXPERTS - 1)], bi_send)
        for which, step in enumerate((1, 3)):
            send_g(step).wait_send()
            send_relay(step).wait_send()
            wait_bytes(bo_all.at[pl.ds(0, EXPERTS * half)], hop_send.at[0, which])
            wait_bytes(lam_all.at[pl.ds(0, EXPERTS * half)], hop_send.at[1, which])
        wait_bytes(bo_all.at[pl.ds(0, (EXPERTS - 1) * piece)], bo_send)
        wait_bytes(lam_all.at[pl.ds(0, (EXPERTS - 1) * piece)], lam_send)
        start_all(rounds[1])
        wait_all(rounds[1])
        scy[y] = total(scx)
        out_copy(1, 0).wait_recv()
        start_all(rounds[2])
        wait_all(rounds[2])
        scores[...] = total(scy)
        out_copy(3, 0).wait_recv()
        for part in range(1, parts):
            out_copy(1, part).wait_recv()
            out_copy(3, part).wait_recv()


def shards(grads, basis_out, basis_in, eigvals, counts, slot_query):
    rows, inner = grads.shape[2:]
    experts, width, piece = basis_out.shape
    short = basis_in.shape[1]
    lanes = inner // 128
    parts = 4
    own_k = experts * 2 * piece
    hbm = pl.BlockSpec(memory_space=pl.ANY)
    smem = pl.BlockSpec(memory_space=pltpu.SMEM)
    dma = pltpu.SemaphoreType.DMA
    out, scores = pl.pallas_call(
        kernel,
        out_shape=(
            jax.ShapeDtypeStruct((2, rows, inner), F32),
            jax.ShapeDtypeStruct((8, 128), F32),
        ),
        in_specs=[hbm, hbm, hbm, hbm, smem, smem],
        out_specs=(hbm, pl.BlockSpec(memory_space=pltpu.VMEM)),
        scratch_shapes=[
            pltpu.VMEM((PLANES, rows, inner), F32),
            pltpu.VMEM((own_k, width), F32),
            pltpu.VMEM((short, experts, inner), F32),
            pltpu.VMEM((experts, lanes * short, 128), F32),
            pltpu.VMEM((PLANES, experts, lanes * short, 128), F32),
            pltpu.VMEM((own_k, inner), F32),
            pltpu.VMEM((PLANES * rows, inner), BF16),
            pltpu.VMEM((PLANES * rows, inner), BF16),
            pltpu.VMEM((width, own_k), BF16),
            pltpu.VMEM((width, own_k), BF16),
            pltpu.VMEM((inner, inner), BF16),
            pltpu.VMEM((inner, inner), BF16),
            pltpu.VMEM((own_k, inner), BF16),
            pltpu.VMEM((own_k, inner), BF16),
            pltpu.VMEM((4, parts, rows // parts, inner), F32),
            pltpu.VMEM((8, inner), F32),
            pltpu.VMEM((4, 8, 128), F32),
            pltpu.VMEM((4, 8, 128), F32),
            pltpu.VMEM((4, 8, 128), F32),
            dma((4,)),
            dma((3,)),
            dma((3,)),
            dma(()),
            dma(()),
            dma((3,)),
            dma((3,)),
            dma(()),
            dma((CHUNKS,)),
            dma(()),
            dma((CHUNKS,)),
            dma((2, 2)),
            dma((2, SIDE_CHUNKS)),
            dma((3, parts)),
            dma((2, parts)),
            dma((parts,)),
            dma((9,)),
            dma((9,)),
        ],
        compiler_params=pltpu.CompilerParams(
            collective_id=0, has_side_effects=True, vmem_limit_bytes=66_000_000
        ),
        name="precondition",
    )(
        grads[0, 0],
        jnp.transpose(basis_out, (0, 2, 1)),
        jnp.transpose(basis_in, (1, 0, 2)),
        eigvals,
        counts,
        slot_query[0],
    )
    live = (counts[0] > 0).astype(F32)
    return ((out[0] + out[1]) * live)[None, None], scores[0, :QUERIES]


def solution(mesh):
    in_specs = (
        P(("layer", "expert"), None, "matrix", None),
        P("layer", None, ("expert", "matrix")),
        P("layer", ("expert", "matrix"), None),
        P("layer", ("expert", "matrix"), None),
        P(("layer", "expert")),
        P(("layer", "expert"), None),
    )
    out_specs = (P(("layer", "expert"), None, "matrix", None), P("layer"))
    return jax.shard_map(shards, mesh=mesh, in_specs=in_specs, out_specs=out_specs, check_vma=False)
```

time: 164 us -> 156 us (0.951)
  Pallas kernels: 156 us -> 149 us
  local copies, waits for them, and re-layouts: 6.11 us -> 1.18 us
  other arithmetic: 0 us -> 3.21 us
    pallas_call x1, Pallas kernels: 156 us -> 149 us  [shards(): pl.pallas_call(kernel, out_shape=(jax.ShapeDtypeStruct((2, rows, inner),...]
    mul x0 -> x1, other arithmetic: none -> 3.21 us  [shards(): return (((out[0] + out[1]) * live)[None, None], scores[0, :QUERIES])]
    unnamed x1 -> x0, local copies, waits for them, and re-layouts: 2.65 us -> none
    reshape x2 -> x0, local copies, waits for them, and re-layouts: 2.15 us -> none  [shards(): basis_in.reshape(experts, short, lanes, 128).transpose(0, 2, 1, 3)]
where the time goes in v2:
time: 156 us; the launch traced here: 155 us
  Pallas kernels  149 us (96%)
  other arithmetic  3.21 us (2%)
  between operations  1.94 us (1%)
    pallas_call x1, Pallas kernels, shards(): pl.pallas_call(kernel, out_shape=(jax.ShapeDtypeStruct((2, rows, inner),...  149 us
    mul x1, other arithmetic, shards(): return (((out[0] + out[1]) * live)[None, None], scores[0, :QUERIES])  3.21 us

profile of v2, /device:TPU:0, one launch (start us, length us, event | category | flops | bytes accessed | tf_op | source)
XLA Modules:
  0.0 155.4 jit_solution(10814139879874993704)
XLA Ops:
  1.9 149.1 %precondition.1 = (f32[2,512,768]{2,1,0:T(8,128)}, f32[8,128]{1,0:T(8,128)}) custom-call(f32[512,768]{1,0:T(8,128)} %bitcast.11, f32[16,32,2048]{2,1,0:T(8,128)} %bitcast.10, f32[12,16,768]{2,1,0:T(8,128)} %bitcast.12, f32[16,32,768]{2,1,0:T(8,128)} %lam.1, s32[1]{0:T(128)S(6)} %copy.8.counts, s32[1]{0:T(128)} %bitcast.9.query), custom_call_target="tpu_custom_call" | custom-call | tf_op jit(solution)/shard_map/precondition/pallas_call | solution.py:390
  151.0 3.2 %multiply_bitcast_fusion = f32[1,1,512,768]{3,2,1,0:T(8,128)} fusion(f32[2,512,768]{2,1,0:T(8,128)} %get-tuple-element.4, f32[]{:T(128)} %bitcast.4), kind=kLoop, calls=%fused_computation | loop fusion | flops 786432 | bytes 4718596 | tf_op jit(solution)/shard_map/mul | solution.py:450
  154.2 1.2 slice_bitcast_fusion

commit v3 on v2

--- a/solution.py
+++ b/solution.py
@@ -20,9 +20,10 @@
     (0, 0), (3, 1), (1, 0), (0, 2), (2, 3), (1, 1), (0, 1), (2, 0),
     (0, 3), (3, 0), (1, 2), (3, 3), (1, 3), (2, 1), (3, 2), (2, 2),
 ]
-OWN_CHUNKS = 2
+OWN_CHUNKS = 4
 SIDE_CHUNKS = 4
 CHUNKS = OWN_CHUNKS + SIDE_CHUNKS
+EARLY = 1
 
 
 def split(x):
@@ -216,14 +217,17 @@
         lam_own.start()
         send_g(2).start()
         send_bi()
-        for s in range(1, EXPERTS):
+        for s in range(1, EARLY):
             send_slot(s, True)
         wait_bi_plane()
         send_relay(2).start()
 
         g_own.wait()
-        for step in (1, 3, 2):
+        for step in (1, 3):
             send_g(step).wait_recv()
+        for s in range(EARLY, EXPERTS):
+            send_slot(s, True)
+        send_g(2).wait_recv()
         for k in range(PLANES):
 
             def to_halves(r, carry, k=k):
@@ -273,28 +277,24 @@
             bo_hi[:, at] = high
             bo_lo[:, at] = low
 
-        def own_chunk(c, carry):
-            @pl.when(c == 0)
+        def next_chunk(i, carry):
+            side = lax.rem(i, 2)
+            c = i // 2
+
+            @pl.when(i == 0)
             def _():
                 wait_bytes(bo_all.at[pl.ds(piece, own_rows - piece)], bo_recv.at[0])
                 wait_bytes(lam_all.at[pl.ds(piece, own_rows - piece)], lam_recv.at[0])
 
-            @pl.when(c > 0)
+            @pl.when(i > 0)
             def _():
-                wait_bytes(bo_all.at[pl.ds(0, own_rows)], bo_recv.at[c])
-                wait_bytes(lam_all.at[pl.ds(0, own_rows)], lam_recv.at[c])
-
-            direction(pl.multiple_of(c * own_rows, own_rows), own_rows)
+                wait_bytes(bo_all.at[pl.ds(0, side_rows)], bo_recv.at[side * OWN_CHUNKS + c])
+                wait_bytes(lam_all.at[pl.ds(0, side_rows)], lam_recv.at[side * OWN_CHUNKS + c])
+
+            direction(pl.multiple_of(side * (EXPERTS * piece) + c * side_rows, side_rows), side_rows)
             return carry
 
-        def side_chunk(c, carry):
-            wait_bytes(bo_all.at[pl.ds(0, side_rows)], bo_recv.at[OWN_CHUNKS + c])
-            wait_bytes(lam_all.at[pl.ds(0, side_rows)], lam_recv.at[OWN_CHUNKS + c])
-            direction(pl.multiple_of(EXPERTS * piece + c * side_rows, side_rows), side_rows)
-            return carry
-
-        lax.fori_loop(0, OWN_CHUNKS, own_chunk, 0)
-        lax.fori_loop(0, SIDE_CHUNKS, side_chunk, 0)
+        lax.fori_loop(0, CHUNKS, next_chunk, 0)
 
         value = jnp.sum(score_acc[...]) / (rows * PLANES * inner)
         value = jnp.where(counts[0] > 0, value, 0.0)

time: 156 us -> 146 us (0.936); the launches traced: 155 us -> 143 us
  Pallas kernels: 149 us -> 137 us
    pallas_call x1, Pallas kernels: 149 us -> 137 us  [shards(): pl.pallas_call(kernel, out_shape=(jax.ShapeDtypeStruct((2, rows, inner),...]
where the time goes in v3:
time: 146 us; the launch traced here: 143 us
  Pallas kernels  137 us (94%)
  other arithmetic  3.21 us (2%)
  between operations  1.94 us (1%)
    pallas_call x1, Pallas kernels, shards(): pl.pallas_call(kernel, out_shape=(jax.ShapeDtypeStruct((2, rows, inner),...  137 us
    mul x1, other arithmetic, shards(): return (((out[0] + out[1]) * live)[None, None], scores[0, :QUERIES])  3.21 us

profile of v3, /device:TPU:0, one launch (start us, length us, event | category | flops | bytes accessed | tf_op | source)
XLA Modules:
  0.0 143.1 jit_solution(10500278638922803079)
XLA Ops:
  1.9 136.8 %precondition.1 = (f32[2,512,768]{2,1,0:T(8,128)}, f32[8,128]{1,0:T(8,128)}) custom-call(f32[512,768]{1,0:T(8,128)} %bitcast.11, f32[16,32,2048]{2,1,0:T(8,128)} %bitcast.10, f32[12,16,768]{2,1,0:T(8,128)} %bitcast.12, f32[16,32,768]{2,1,0:T(8,128)} %lam.1, s32[1]{0:T(128)S(6)} %copy.8.counts, s32[1]{0:T(128)} %bitcast.9.query), custom_call_target="tpu_custom_call" | custom-call | tf_op jit(solution)/shard_map/precondition/pallas_call | solution.py:390
  138.7 3.2 %multiply_bitcast_fusion = f32[1,1,512,768]{3,2,1,0:T(8,128)} fusion(f32[2,512,768]{2,1,0:T(8,128)} %get-tuple-element.4, f32[]{:T(128)} %bitcast.4), kind=kLoop, calls=%fused_computation | loop fusion | flops 786432 | bytes 4718596 | tf_op jit(solution)/shard_map/mul | solution.py:450
  142.0 1.2 slice_bitcast_fusion

commit v4 on v3

--- a/solution.py
+++ b/solution.py
@@ -103,19 +103,30 @@
             device_id_type=MESH,
         )
 
+    pl.semaphore_wait(barrier, len(partners))
+
+    steps = {1: 0, 3: 1, 2: 2}
+
+    def send_g(step):
+        return remote(g, g_all.at[m], g_send.at[steps[step]], g_recv.at[steps[step]], e, plane(step))
+
+    g_own = pltpu.make_async_copy(g, g_all.at[m], loc_sem.at[1])
+
+    @pl.when(active)
+    def _():
+        g_own.start()
+        send_g(2).start()
+
+    @pl.when(jnp.logical_not(active))
+    def _():
+        send_g(1).start()
+        send_g(3).start()
+
     bi_in.wait()
     for to in range(EXPERTS):
         for c in range(lanes):
             bi_stage[to, pl.ds(c * short, short), :] = bi_raw[:, to, pl.ds(c * 128, 128)]
 
-    pl.semaphore_wait(barrier, len(partners))
-
-    steps = {1: 0, 3: 1, 2: 2}
-
-    def send_g(step):
-        return remote(g, g_all.at[m], g_send.at[steps[step]], g_recv.at[steps[step]], e, plane(step))
-
-    g_own = pltpu.make_async_copy(g, g_all.at[m], loc_sem.at[1])
     bo_own = pltpu.make_async_copy(bo.at[e], bo_all.at[pl.ds(0, piece)], loc_sem.at[2])
     lam_own = pltpu.make_async_copy(lam.at[e], lam_all.at[pl.ds(0, piece)], loc_sem.at[3])
 
@@ -212,10 +223,8 @@
 
     @pl.when(active)
     def _():
-        g_own.start()
         bo_own.start()
         lam_own.start()
-        send_g(2).start()
         send_bi()
         for s in range(1, EARLY):
             send_slot(s, True)
@@ -278,15 +287,15 @@
             bo_lo[:, at] = low
 
         def next_chunk(i, carry):
-            side = lax.rem(i, 2)
+            side = lax.rem(i + 1, 2)
             c = i // 2
 
-            @pl.when(i == 0)
+            @pl.when(i == 1)
             def _():
                 wait_bytes(bo_all.at[pl.ds(piece, own_rows - piece)], bo_recv.at[0])
                 wait_bytes(lam_all.at[pl.ds(piece, own_rows - piece)], lam_recv.at[0])
 
-            @pl.when(i > 0)
+            @pl.when(i != 1)
             def _():
                 wait_bytes(bo_all.at[pl.ds(0, side_rows)], bo_recv.at[side * OWN_CHUNKS + c])
                 wait_bytes(lam_all.at[pl.ds(0, side_rows)], lam_recv.at[side * OWN_CHUNKS + c])
@@ -342,8 +351,6 @@
     @pl.when(jnp.logical_not(active))
     def _():
         scz[m] = jnp.zeros((8, 128), F32)
-        send_g(1).start()
-        send_g(3).start()
         send_bi()
         for s in range(EXPERTS):
             send_slot(s, False)

time: 146 us -> 142 us (0.973); the launches traced: 143 us -> 141 us
  Pallas kernels: 137 us -> 135 us
    pallas_call x1, Pallas kernels: 137 us -> 135 us  [shards(): pl.pallas_call(kernel, out_shape=(jax.ShapeDtypeStruct((2, rows, inner),...]
where the time goes in v4:
time: 142 us; the launch traced here: 141 us
  Pallas kernels  135 us (95%)
  other arithmetic  3.21 us (2%)
  between operations  1.94 us (1%)
    pallas_call x1, Pallas kernels, shards(): pl.pallas_call(kernel, out_shape=(jax.ShapeDtypeStruct((2, rows, inner),...  135 us
    mul x1, other arithmetic, shards(): return (((out[0] + out[1]) * live)[None, None], scores[0, :QUERIES])  3.21 us

profile of v4, /device:TPU:0, one launch (start us, length us, event | category | flops | bytes accessed | tf_op | source)
XLA Modules:
  0.0 141.4 jit_solution(14284894903641453765)
XLA Ops:
  1.9 135.1 %precondition.1 = (f32[2,512,768]{2,1,0:T(8,128)}, f32[8,128]{1,0:T(8,128)}) custom-call(f32[512,768]{1,0:T(8,128)} %bitcast.11, f32[16,32,2048]{2,1,0:T(8,128)} %bitcast.10, f32[12,16,768]{2,1,0:T(8,128)} %bitcast.12, f32[16,32,768]{2,1,0:T(8,128)} %lam.1, s32[1]{0:T(128)S(6)} %copy.8.counts, s32[1]{0:T(128)} %bitcast.9.query), custom_call_target="tpu_custom_call" | custom-call | tf_op jit(solution)/shard_map/precondition/pallas_call | solution.py:397
  137.0 3.2 %multiply_bitcast_fusion = f32[1,1,512,768]{3,2,1,0:T(8,128)} fusion(f32[2,512,768]{2,1,0:T(8,128)} %get-tuple-element.4, f32[]{:T(128)} %bitcast.4), kind=kLoop, calls=%fused_computation | loop fusion | flops 786432 | bytes 4718596 | tf_op jit(solution)/shard_map/mul | solution.py:457
  140.2 1.2 slice_bitcast_fusion

commit v5 on v4

--- a/solution.py
+++ b/solution.py
@@ -23,6 +23,7 @@
 OWN_CHUNKS = 4
 SIDE_CHUNKS = 4
 CHUNKS = OWN_CHUNKS + SIDE_CHUNKS
+HOPS = 8
 EARLY = 1
 
 
@@ -33,10 +34,6 @@
 
 def dot(a, b):
     return lax.dot_general(a, b, (((1,), (0,)), ((), ())), preferred_element_type=F32)
-
-
-def dot_t(a, b):
-    return lax.dot_general(a, b, (((1,), (1,)), ((), ())), preferred_element_type=F32)
 
 
 def wait_bytes(ref, sem):
@@ -51,7 +48,7 @@
 
 def kernel(
     g, bo, bi, lam, counts, query, out, scores,
-    g_all, bo_all, bi_raw, bi_stage, bi_all, lam_all, g_hi, g_lo, bo_hi, bo_lo, bi_hi, bi_lo,
+    g_all, bo_all, bi_raw, bi_stage, bi_all, lam_all, g_hi, g_lo, bo_hi, bo_lo, bi_hi, bi_lo, bit_hi, bit_lo,
     back_hi, back_lo, snd, score_acc, scz, scx, scy,
     loc_sem, g_send, g_recv, bi_send, bi_recv, rel_send, rel_recv,
     bo_send, bo_recv, lam_send, lam_recv, hop_send, hop_recv, out_send, out_recv, own_sem,
@@ -143,33 +140,36 @@
             remote(bo.at[to], bo_all.at[there], bo_send, bo_recv.at[chunk], to, m).start()
             remote(lam.at[to], lam_all.at[there], lam_send, lam_recv.at[chunk], to, m).start()
         else:
-            chunk = s * SIDE_CHUNKS // EXPERTS
+            group = s * HOPS // EXPERTS
             for which in range(2):
                 mine = pl.ds(which * half, half)
                 there = pl.ds((which * EXPERTS + s) * half, half)
                 if s:
-                    remote(bo.at[to, mine], bo_all.at[there], bo_send, hop_recv.at[0, chunk], to, m).start()
-                    remote(lam.at[to, mine], lam_all.at[there], lam_send, hop_recv.at[1, chunk], to, m).start()
+                    remote(bo.at[to, mine], bo_all.at[there], bo_send, hop_recv.at[0, group], to, m).start()
+                    remote(lam.at[to, mine], lam_all.at[there], lam_send, hop_recv.at[1, group], to, m).start()
                 else:
                     pltpu.make_async_copy(bo.at[e, mine], bo_all.at[there], loc_sem.at[which]).start()
                     pltpu.make_async_copy(lam.at[e, mine], lam_all.at[there], loc_sem.at[2 + which]).start()
 
-    def wait_slots(chunk):
-        ready = side_rows
-        if chunk == 0:
+    hop_rows = EXPERTS * half // HOPS
+
+    def wait_slots(group):
+        ready = 2 * hop_rows
+        if group == 0:
             ready -= piece
             for which in range(2):
                 wait_bytes(bo_all.at[pl.ds(0, half)], loc_sem.at[which])
                 wait_bytes(lam_all.at[pl.ds(0, half)], loc_sem.at[2 + which])
-        wait_bytes(bo_all.at[pl.ds(0, ready)], hop_recv.at[0, chunk])
-        wait_bytes(lam_all.at[pl.ds(0, ready)], hop_recv.at[1, chunk])
-
-    def hand_on(chunk):
-        count = side_rows // 2
+        wait_bytes(bo_all.at[pl.ds(0, ready)], hop_recv.at[0, group])
+        wait_bytes(lam_all.at[pl.ds(0, ready)], hop_recv.at[1, group])
+
+    def hand_on(group):
+        chunk, place_in = divmod(group, HOPS // SIDE_CHUNKS)
+        at = OWN_CHUNKS + chunk
         for which, step in enumerate((1, 3)):
-            here = pl.ds(which * EXPERTS * half + chunk * count, count)
-            there = pl.ds(EXPERTS * piece + chunk * side_rows + which * count, count)
-            at = OWN_CHUNKS + chunk
+            here = pl.ds(which * EXPERTS * half + group * hop_rows, hop_rows)
+            start = EXPERTS * piece + chunk * side_rows + which * (side_rows // 2) + place_in * hop_rows
+            there = pl.ds(start, hop_rows)
             remote(bo_all.at[here], bo_all.at[there], hop_send.at[0, which], bo_recv.at[at], e, plane(step)).start()
             remote(lam_all.at[here], lam_all.at[there], hop_send.at[1, which], lam_recv.at[at], e, plane(step)).start()
 
@@ -264,6 +264,8 @@
             return carry
 
         lax.fori_loop(0, EXPERTS, unpack, 0)
+        bit_hi[...] = jnp.transpose(bi_hi[...])
+        bit_lo[...] = jnp.transpose(bi_lo[...])
 
         score_acc[...] = jnp.zeros_like(score_acc)
         bo_own.wait()
@@ -279,7 +281,7 @@
             scaled = turned / (lam_all[at, :] + DAMPING)
             score_acc[...] += jnp.sum((turned * scaled).reshape(-1, 8, inner), axis=0)
             high, low = split(scaled)
-            high, low = split(three_pass(dot_t, high, low, bi_hi[...], bi_lo[...]))
+            high, low = split(three_pass(dot, high, low, bit_hi[...], bit_lo[...]))
             back_hi[at, :] = high
             back_lo[at, :] = low
             high, low = split(jnp.transpose(columns))
@@ -334,7 +336,7 @@
             own_copy(part - 1).start()
         start_all(rounds[2])
         wait_all(rounds[2])
-        scores[...] = total(scy)
+        scores[...] = total(scy)[0:1, :QUERIES]
         own_copy(parts - 1).start()
 
         wait_bytes(bi_stage.at[pl.ds(0, EXPERTS - 1)], bi_send)
@@ -357,9 +359,9 @@
         wait_bi_plane()
         send_relay(1).start()
         send_relay(3).start()
-        for chunk in range(SIDE_CHUNKS):
-            wait_slots(chunk)
-            hand_on(chunk)
+        for group in range(HOPS):
+            wait_slots(group)
+            hand_on(group)
         start_all(rounds[0])
         wait_all(rounds[0])
         scx[x] = total(scz)
@@ -377,7 +379,7 @@
         out_copy(1, 0).wait_recv()
         start_all(rounds[2])
         wait_all(rounds[2])
-        scores[...] = total(scy)
+        scores[...] = total(scy)[0:1, :QUERIES]
         out_copy(3, 0).wait_recv()
         for part in range(1, parts):
             out_copy(1, part).wait_recv()
@@ -398,7 +400,7 @@
         kernel,
         out_shape=(
             jax.ShapeDtypeStruct((2, rows, inner), F32),
-            jax.ShapeDtypeStruct((8, 128), F32),
+            jax.ShapeDtypeStruct((1, QUERIES), F32),
         ),
         in_specs=[hbm, hbm, hbm, hbm, smem, smem],
         out_specs=(hbm, pl.BlockSpec(memory_space=pltpu.VMEM)),
@@ -413,6 +415,8 @@
             pltpu.VMEM((PLANES * rows, inner), BF16),
             pltpu.VMEM((width, own_k), BF16),
             pltpu.VMEM((width, own_k), BF16),
+            pltpu.VMEM((inner, inner), BF16),
+            pltpu.VMEM((inner, inner), BF16),
             pltpu.VMEM((inner, inner), BF16),
             pltpu.VMEM((inner, inner), BF16),
             pltpu.VMEM((own_k, inner), BF16),
@@ -434,7 +438,7 @@
             dma(()),
             dma((CHUNKS,)),
             dma((2, 2)),
-            dma((2, SIDE_CHUNKS)),
+            dma((2, HOPS)),
             dma((3, parts)),
             dma((2, parts)),
             dma((parts,)),
@@ -454,7 +458,7 @@
         slot_query[0],
     )
     live = (counts[0] > 0).astype(F32)
-    return ((out[0] + out[1]) * live)[None, None], scores[0, :QUERIES]
+    return ((out[0] + out[1]) * live)[None, None], scores[0]
 
 
 def solution(mesh):

time: 142 us -> 141 us (level)
  no operation moved by 1% of the time
where the time goes in v5:
time: 141 us
  Pallas kernels  135 us (96%)
  other arithmetic  3.21 us (2%)
  between operations  1.94 us (1%)
    pallas_call x1, Pallas kernels, shards(): pl.pallas_call(kernel, out_shape=(jax.ShapeDtypeStruct((2, rows, inner),...  135 us
    mul x1, other arithmetic, shards(): return (((out[0] + out[1]) * live)[None, None], scores[0])  3.21 us

profile of v5, /device:TPU:0, one launch (start us, length us, event | category | flops | bytes accessed | tf_op | source)
XLA Modules:
  0.0 140.5 jit_solution(1116287854884915695)
XLA Ops:
  1.9 134.9 %precondition.1 = (f32[2,512,768]{2,1,0:T(8,128)}, f32[1,32]{1,0:T(1,128)}) custom-call(f32[512,768]{1,0:T(8,128)} %bitcast.10, f32[16,32,2048]{2,1,0:T(8,128)} %bitcast.9, f32[12,16,768]{2,1,0:T(8,128)} %bitcast.11, f32[16,32,768]{2,1,0:T(8,128)} %lam.1, s32[1]{0:T(128)S(6)} %copy.9.counts, s32[1]{0:T(128)} %bitcast.8.query), custom_call_target="tpu_custom_call" | custom-call | tf_op jit(solution)/shard_map/precondition/pallas_call | solution.py:399
  136.8 0.0 copy-start
  136.8 3.2 %multiply_bitcast_fusion = f32[1,1,512,768]{3,2,1,0:T(8,128)} fusion(f32[2,512,768]{2,1,0:T(8,128)} %get-tuple-element.4, f32[]{:T(128)} %bitcast.4), kind=kLoop, calls=%fused_computation | loop fusion | flops 786432 | bytes 4718596 | tf_op jit(solution)/shard_map/mul | solution.py:461
  140.0 0.0 copy-done
  140.0 0.5 copy.11
Async XLA Ops:
  136.8 3.2 %copy-start = (f32[1,32]{1,0:T(1,128)S(1)}, f32[1,32]{1,0:T(1,128)}, u32[]{:S(2)}) copy-start(f32[1,32]{1,0:T(1,128)} %get-tuple-element.5) | copy-start | bytes 388
